TPU v7x, 32 devices: a whole 2x2x4 slice. The times are simulated.
32 devices in a mesh: mem: 4 (over z), lat: 8 (over y, x, core).
Axes of the slice: x: 2, y: 2, z: 4, core: 2. Of those that a mesh axis runs over, the one named last changes fastest.
Arguments:
- ensemble: bfloat16 [32, 72, 8, 1440], P('mem', None, 'lat'), may hold values from -6 to 6
- truth: bfloat16 [72, 8, 1440], P(None, 'lat'), may hold values from -6 to 6
- row_weight: float32 [8], P('lat'), may hold values from 0.3 to 7, as said below
Outputs:
- loss: float32 [], replicated
- gradient: bfloat16 [32, 72, 8, 1440], P('mem', None, 'lat')
Inputs may be any that keep to these rules, and one draw needn't show every extreme that they name: `row_weight`: positive.
All inputs are finite; a program needn't handle non-finite values.
Results may differ from a plain program's by a relative error of at most 0.003.
Values may be sent and summed in bfloat16 or wider, within the bound.
No kernel may reach another device: no remote copies, remote signals or barrier semaphores. Data moves between devices by JAX's collectives and lax.ppermute only.
A program may use at most 128 MiB of HBM per device.

v0:
```python
import jax
import jax.numpy as jnp
from jax import lax
from jax.sharding import PartitionSpec as P


def pair_terms(left, right):
    count_left = left.shape[0]
    grouped = left.reshape((count_left // 2, 2) + left.shape[1:])

    def one_group(block):
        diff = block[:, None] - right[None]
        return (jnp.sum(jnp.abs(diff), axis=1), jnp.sum(jnp.sign(diff), axis=1))

    spread, count = lax.map(one_group, grouped)
    return (spread.reshape(left.shape), count.reshape(left.shape))


def finish(values, target, weight, spread, count, members):
    skill = values - target
    cell = jnp.sum(jnp.abs(skill), axis=0) / members - jnp.sum(spread, axis=0) / (
        2.0 * members * (members - 1)
    )
    partial_value = jnp.sum(weight[None, :, None] * cell)
    grad = (weight[None, None, :, None] * (jnp.sign(skill) - count / (members - 1))).astype(
        jnp.bfloat16
    )
    return (partial_value, grad)


def on_device(ensemble, truth, row_weight):
    local_members, channels, rows, cells = ensemble.shape
    groups = lax.axis_size("mem")
    members = local_members * groups
    regrouped = lax.all_to_all(ensemble, "mem", split_axis=1, concat_axis=0, tiled=True)
    share = channels // groups
    start = lax.axis_index("mem") * share
    target = lax.dynamic_slice_in_dim(truth, start, share, 0).astype(jnp.float32)
    values = regrouped.astype(jnp.float32)
    spread, count = pair_terms(values, values)
    partial_value, grad = finish(values, target[None], row_weight, spread, count, members)
    gradient = lax.all_to_all(grad, "mem", split_axis=0, concat_axis=1, tiled=True)
    total = lax.psum(partial_value, ("mem", "lat"))
    loss = total / (channels * rows * lax.axis_size("lat") * cells)
    return (loss, gradient)


def solution(mesh):
    placed = (P("mem", None, "lat", None), P(None, "lat", None), P("lat"))
    return jax.shard_map(
        on_device,
        mesh=mesh,
        in_specs=placed,
        out_specs=(P(), P("mem", None, "lat", None)),
        check_vma=False,
    )
```

profile of v0, /device:TPU:0, one launch (start us, length us, event | category | flops | bytes accessed | tf_op | source)
XLA Modules:
  0.0 257.8 jit_solution(14661055803289279704)
XLA Ops:
  0.6 3.2 %copy.40 = bf16[8,72,1,1440]{3,0,2,1:T(8,128)(2,1)} copy(bf16[8,72,1,1440]{3,1,2,0:T(8,128)(2,1)} %param.5) | data formatting | bytes 3317760 | tf_op args[0]
  3.8 6.3 %all-to-all-start = ((bf16[8,72,1,1440]{3,0,2,1:T(8,128)(2,1)}), bf16[8,72,1,1440]{3,0,2,1:T(8,128)(2,1)S(1)}, u32[]{:S(2)}, u32[]{:S(2)}) async-start(bf16[8,72,1,1440]{3,0,2,1:T(8,128)(2,1)} %copy.40), calls=%async_computation | async-start | bytes 3538944 | tf_op jit(solution)/shard_map/all_to_all | solution.py:35
  10.8 1.6 bitcast_convert_fusion
  12.4 38.9 %all-to-all-done = bf16[8,72,1,1440]{3,0,2,1:T(8,128)(2,1)S(1)} async-done(((bf16[8,72,1,1440]{3,0,2,1:T(8,128)(2,1)}), bf16[8,72,1,1440]{3,0,2,1:T(8,128)(2,1)S(1)}, u32[]{:S(2)}, u32[]{:S(2)}) %all-to-all-start) | async-done | bytes 1658912 | tf_op jit(solution)/shard_map/all_to_all | solution.py:35
  51.4 1.2 copy-done
  53.0 1.9 copy_bitcast_fusion.1
  55.0 5.4 %copy.42 = f32[4,8,18,1,1440]{4,3,2,1,0:T(1,128)} copy(f32[4,8,18,1,1440]{4,1,2,0,3:T(8,128)S(1)} %convert_bitcast_fusion) | data formatting | bytes 6635520 | tf_op jit(solution)/shard_map/convert_element_type | solution.py:39
  60.4 94.5 %while.12 = (s32[]{:T(128)}, f32[16,2,18,1,1440]{4,1,2,3,0:T(2,128)}, f32[16,2,18,1,1440]{4,1,2,3,0:T(2,128)}, f32[16,2,18,1,1440]{4,3,2,1,0:T(1,128)}, f32[32,18,1,1440]{3,0,2,1:T(8,128)S(1)}, /*index=5*/s32[]{:T(128)}) while((s32[]{:T(128)}, f32[16,2,18,1,1440]{4,1,2,3,0:T(2,128)}, f32[16,2,18,1,1440]{4,1,2,3,0:T(2,128)}, ...), condition=%wide.region_4.5_spmd, body=%wide.region_1.4_spmd.sunk | while | flops 8190722 | bytes 6041673 | solution.py:15
  60.4 1.0 constant_dynamic-slice_fusion.2
  61.5 3.6 %fusion.9 = (f32[2,18,1440]{2,1,0:T(8,128)S(1)}, f32[2,18,1440]{2,1,0:T(8,128)S(1)}) fusion(f32[32,18,1440]{2,0,1:T(8,128)S(1)} %bitcast.50, f32[2,18,1440]{2,1,0:T(8,128)S(1)} %copy.65), kind=kLoop, calls=%fused_computation.3.clone.1 | loop fusion | flops 8190720 | bytes 3939840 | tf_op jit(solution)/shard_map/while/body/eval_jaxpr/reduce_sum | solution.py:13
  65.1 1.1 bitcast_dynamic-update-slice_fusion.3
  66.3 1.0 constant_dynamic-slice_fusion.2
  67.4 3.6 %fusion.9 = (f32[2,18,1440]{2,1,0:T(8,128)S(1)}, f32[2,18,1440]{2,1,0:T(8,128)S(1)}) fusion(f32[32,18,1440]{2,0,1:T(8,128)S(1)} %bitcast.50, f32[2,18,1440]{2,1,0:T(8,128)S(1)} %copy.65), kind=kLoop, calls=%fused_computation.3.clone.1 | loop fusion | flops 8190720 | bytes 3939840 | tf_op jit(solution)/shard_map/while/body/eval_jaxpr/reduce_sum | solution.py:13
  71.0 1.1 bitcast_dynamic-update-slice_fusion.3
  72.2 1.0 constant_dynamic-slice_fusion.2
  73.3 3.6 %fusion.9 = (f32[2,18,1440]{2,1,0:T(8,128)S(1)}, f32[2,18,1440]{2,1,0:T(8,128)S(1)}) fusion(f32[32,18,1440]{2,0,1:T(8,128)S(1)} %bitcast.50, f32[2,18,1440]{2,1,0:T(8,128)S(1)} %copy.65), kind=kLoop, calls=%fused_computation.3.clone.1 | loop fusion | flops 8190720 | bytes 3939840 | tf_op jit(solution)/shard_map/while/body/eval_jaxpr/reduce_sum | solution.py:13
  77.0 1.1 bitcast_dynamic-update-slice_fusion.3
  78.1 1.0 constant_dynamic-slice_fusion.2
  79.2 3.6 %fusion.9 = (f32[2,18,1440]{2,1,0:T(8,128)S(1)}, f32[2,18,1440]{2,1,0:T(8,128)S(1)}) fusion(f32[32,18,1440]{2,0,1:T(8,128)S(1)} %bitcast.50, f32[2,18,1440]{2,1,0:T(8,128)S(1)} %copy.65), kind=kLoop, calls=%fused_computation.3.clone.1 | loop fusion | flops 8190720 | bytes 3939840 | tf_op jit(solution)/shard_map/while/body/eval_jaxpr/reduce_sum | solution.py:13
  82.9 1.1 bitcast_dynamic-update-slice_fusion.3
  84.0 1.0 constant_dynamic-slice_fusion.2
  85.1 3.6 %fusion.9 = (f32[2,18,1440]{2,1,0:T(8,128)S(1)}, f32[2,18,1440]{2,1,0:T(8,128)S(1)}) fusion(f32[32,18,1440]{2,0,1:T(8,128)S(1)} %bitcast.50, f32[2,18,1440]{2,1,0:T(8,128)S(1)} %copy.65), kind=kLoop, calls=%fused_computation.3.clone.1 | loop fusion | flops 8190720 | bytes 3939840 | tf_op jit(solution)/shard_map/while/body/eval_jaxpr/reduce_sum | solution.py:13
  88.8 1.1 bitcast_dynamic-update-slice_fusion.3
  89.9 1.0 constant_dynamic-slice_fusion.2
  91.0 3.6 %fusion.9 = (f32[2,18,1440]{2,1,0:T(8,128)S(1)}, f32[2,18,1440]{2,1,0:T(8,128)S(1)}) fusion(f32[32,18,1440]{2,0,1:T(8,128)S(1)} %bitcast.50, f32[2,18,1440]{2,1,0:T(8,128)S(1)} %copy.65), kind=kLoop, calls=%fused_computation.3.clone.1 | loop fusion | flops 8190720 | bytes 3939840 | tf_op jit(solution)/shard_map/while/body/eval_jaxpr/reduce_sum | solution.py:13
  94.7 1.1 bitcast_dynamic-update-slice_fusion.3
  95.8 1.0 constant_dynamic-slice_fusion.2
  96.9 3.6 %fusion.9 = (f32[2,18,1440]{2,1,0:T(8,128)S(1)}, f32[2,18,1440]{2,1,0:T(8,128)S(1)}) fusion(f32[32,18,1440]{2,0,1:T(8,128)S(1)} %bitcast.50, f32[2,18,1440]{2,1,0:T(8,128)S(1)} %copy.65), kind=kLoop, calls=%fused_computation.3.clone.1 | loop fusion | flops 8190720 | bytes 3939840 | tf_op jit(solution)/shard_map/while/body/eval_jaxpr/reduce_sum | solution.py:13
  100.6 1.2 bitcast_dynamic-update-slice_fusion.3
  101.7 1.0 constant_dynamic-slice_fusion.2
  102.8 3.6 %fusion.9 = (f32[2,18,1440]{2,1,0:T(8,128)S(1)}, f32[2,18,1440]{2,1,0:T(8,128)S(1)}) fusion(f32[32,18,1440]{2,0,1:T(8,128)S(1)} %bitcast.50, f32[2,18,1440]{2,1,0:T(8,128)S(1)} %copy.65), kind=kLoop, calls=%fused_computation.3.clone.1 | loop fusion | flops 8190720 | bytes 3939840 | tf_op jit(solution)/shard_map/while/body/eval_jaxpr/reduce_sum | solution.py:13
  106.5 1.1 bitcast_dynamic-update-slice_fusion.3
  107.6 1.0 constant_dynamic-slice_fusion.2
  108.8 3.6 %fusion.9 = (f32[2,18,1440]{2,1,0:T(8,128)S(1)}, f32[2,18,1440]{2,1,0:T(8,128)S(1)}) fusion(f32[32,18,1440]{2,0,1:T(8,128)S(1)} %bitcast.50, f32[2,18,1440]{2,1,0:T(8,128)S(1)} %copy.65), kind=kLoop, calls=%fused_computation.3.clone.1 | loop fusion | flops 8190720 | bytes 3939840 | tf_op jit(solution)/shard_map/while/body/eval_jaxpr/reduce_sum | solution.py:13
  112.4 1.1 bitcast_dynamic-update-slice_fusion.3
  113.5 1.0 constant_dynamic-slice_fusion.2
  114.7 3.6 %fusion.9 = (f32[2,18,1440]{2,1,0:T(8,128)S(1)}, f32[2,18,1440]{2,1,0:T(8,128)S(1)}) fusion(f32[32,18,1440]{2,0,1:T(8,128)S(1)} %bitcast.50, f32[2,18,1440]{2,1,0:T(8,128)S(1)} %copy.65), kind=kLoop, calls=%fused_computation.3.clone.1 | loop fusion | flops 8190720 | bytes 3939840 | tf_op jit(solution)/shard_map/while/body/eval_jaxpr/reduce_sum | solution.py:13
  118.3 1.1 bitcast_dynamic-update-slice_fusion.3
  119.5 1.0 constant_dynamic-slice_fusion.2
  120.6 3.6 %fusion.9 = (f32[2,18,1440]{2,1,0:T(8,128)S(1)}, f32[2,18,1440]{2,1,0:T(8,128)S(1)}) fusion(f32[32,18,1440]{2,0,1:T(8,128)S(1)} %bitcast.50, f32[2,18,1440]{2,1,0:T(8,128)S(1)} %copy.65), kind=kLoop, calls=%fused_computation.3.clone.1 | loop fusion | flops 8190720 | bytes 3939840 | tf_op jit(solution)/shard_map/while/body/eval_jaxpr/reduce_sum | solution.py:13
  124.2 1.1 bitcast_dynamic-update-slice_fusion.3
  125.4 1.0 constant_dynamic-slice_fusion.2
  126.5 3.6 %fusion.9 = (f32[2,18,1440]{2,1,0:T(8,128)S(1)}, f32[2,18,1440]{2,1,0:T(8,128)S(1)}) fusion(f32[32,18,1440]{2,0,1:T(8,128)S(1)} %bitcast.50, f32[2,18,1440]{2,1,0:T(8,128)S(1)} %copy.65), kind=kLoop, calls=%fused_computation.3.clone.1 | loop fusion | flops 8190720 | bytes 3939840 | tf_op jit(solution)/shard_map/while/body/eval_jaxpr/reduce_sum | solution.py:13
  130.1 1.1 bitcast_dynamic-update-slice_fusion.3
  132.4 3.6 %fusion.9 = (f32[2,18,1440]{2,1,0:T(8,128)S(1)}, f32[2,18,1440]{2,1,0:T(8,128)S(1)}) fusion(f32[32,18,1440]{2,0,1:T(8,128)S(1)} %bitcast.50, f32[2,18,1440]{2,1,0:T(8,128)S(1)} %copy.65), kind=kLoop, calls=%fused_computation.3.clone.1 | loop fusion | flops 8190720 | bytes 3939840 | tf_op jit(solution)/shard_map/while/body/eval_jaxpr/reduce_sum | solution.py:13
  136.0 1.1 bitcast_dynamic-update-slice_fusion.3
  137.1 1.0 constant_dynamic-slice_fusion.2
  138.3 3.6 %fusion.9 = (f32[2,18,1440]{2,1,0:T(8,128)S(1)}, f32[2,18,1440]{2,1,0:T(8,128)S(1)}) fusion(f32[32,18,1440]{2,0,1:T(8,128)S(1)} %bitcast.50, f32[2,18,1440]{2,1,0:T(8,128)S(1)} %copy.65), kind=kLoop, calls=%fused_computation.3.clone.1 | loop fusion | flops 8190720 | bytes 3939840 | tf_op jit(solution)/shard_map/while/body/eval_jaxpr/reduce_sum | solution.py:13
  141.9 1.1 bitcast_dynamic-update-slice_fusion.3
  144.2 3.6 %fusion.9 = (f32[2,18,1440]{2,1,0:T(8,128)S(1)}, f32[2,18,1440]{2,1,0:T(8,128)S(1)}) fusion(f32[32,18,1440]{2,0,1:T(8,128)S(1)} %bitcast.50, f32[2,18,1440]{2,1,0:T(8,128)S(1)} %copy.65), kind=kLoop, calls=%fused_computation.3.clone.1 | loop fusion | flops 8190720 | bytes 3939840 | tf_op jit(solution)/shard_map/while/body/eval_jaxpr/reduce_sum | solution.py:13
  147.8 1.1 bitcast_dynamic-update-slice_fusion.3
  148.9 1.0 constant_dynamic-slice_fusion.2
  150.1 3.6 %fusion.9 = (f32[2,18,1440]{2,1,0:T(8,128)S(1)}, f32[2,18,1440]{2,1,0:T(8,128)S(1)}) fusion(f32[32,18,1440]{2,0,1:T(8,128)S(1)} %bitcast.50, f32[2,18,1440]{2,1,0:T(8,128)S(1)} %copy.65), kind=kLoop, calls=%fused_computation.3.clone.1 | loop fusion | flops 8190720 | bytes 3939840 | tf_op jit(solution)/shard_map/while/body/eval_jaxpr/reduce_sum | solution.py:13
  153.7 1.1 bitcast_dynamic-update-slice_fusion.3
  154.8 3.8 %broadcast_multiply_fusion = f32[16,2,18,1,1440]{4,1,2,3,0:T(2,128)S(1)} fusion(f32[16,2,18,1,1440]{4,1,2,3,0:T(2,128)} %get-tuple-element.31), kind=kLoop, calls=%fused_computation.19 | loop fusion | flops 829440 | bytes 6635520 | tf_op jit(solution)/shard_map/div | solution.py:25
  158.7 3.7 %copy.46 = f32[16,2,18,1,1440]{4,1,0,2,3:T(2,128)} copy(f32[16,2,18,1,1440]{4,1,2,3,0:T(2,128)S(1)} %broadcast_multiply_fusion) | data formatting | bytes 6635520 | tf_op jit(solution)/shard_map/div | solution.py:25
  162.4 5.6 %div.30 = f32[32,18,1,1440]{3,0,1,2:T(8,128)} reshape(f32[16,2,18,1,1440]{4,1,0,2,3:T(2,128)} %copy.46) | data formatting | bytes 6635520 | tf_op jit(solution)/shard_map/div | solution.py:25
  168.0 3.3 %fusion.7 = bf16[32,18,1,1440]{3,0,1,2:T(8,128)(2,1)S(1)} fusion(f32[32,18,1,1440]{3,0,1,2:T(8,128)} %div.30, f32[18,1440]{1,0:T(8,128)S(1)} %copy-done.2, f32[]{:T(128)} %bitcast.49, bf16[8,4,18,1,1440]{4,0,2,1,3:T(8,128)(2,1)S(1)} %bitcast.53), kind=kLoop, calls=%fused_computation.16 | loop fusion | flops 4976640 | bytes 6739204 | tf_op jit(solution)/shard_map/convert_element_type | solution.py:25
  171.3 2.5 copy.47
  173.8 4.5 %all-to-all-start.1 = ((bf16[32,18,1,1440]{3,1,2,0:T(8,128)(2,1)}), bf16[32,18,1,1440]{3,1,2,0:T(8,128)(2,1)}, u32[]{:S(2)}, u32[]{:S(2)}) async-start(bf16[32,18,1,1440]{3,1,2,0:T(8,128)(2,1)} %copy.47), calls=%async_computation.1 | async-start | bytes 4718592 | tf_op jit(solution)/shard_map/all_to_all | solution.py:42
  178.3 3.1 %reduce_sum.46 = f32[18,1440]{1,0:T(8,128)S(1)} reduce(f32[16,2,18,1,1440]{4,1,2,3,0:T(2,128)} %get-tuple-element.30, f32[]{:T(128)} %constant.33.clone.1), dimensions={0,1,3}, to_apply=%region_5.6 | reduce | flops 803520 | bytes 3421444 | tf_op jit(solution)/shard_map/reduce_sum | solution.py:21
  182.7 69.2 %psum.7 = f32[]{:T(128)} all-reduce(f32[]{:T(128)} %multiply_reduce_fusion), channel_id=1, replica_groups=mesh['mem'=4,'lat'=8] {'mem','lat'}, use_global_device_ids=true, to_apply=%region_7.8 | all-reduce | flops 1 | bytes 8 | tf_op jit(solution)/shard_map/psum | solution.py:43
  252.6 2.2 copy.59
  255.0 1.7 copy.50
  (46 shorter events, 6.4 us)
Async XLA Ops:
  3.8 47.5 %all-to-all-start = ((bf16[8,72,1,1440]{3,0,2,1:T(8,128)(2,1)}), bf16[8,72,1,1440]{3,0,2,1:T(8,128)(2,1)S(1)}, u32[]{:S(2)}, u32[]{:S(2)}) async-start(bf16[8,72,1,1440]{3,0,2,1:T(8,128)(2,1)} %copy.40), calls=%async_computation | async-start | bytes 3538944 | tf_op jit(solution)/shard_map/all_to_all | solution.py:35
  51.3 1.2 copy-start
  162.4 5.6 %copy-start.1 = (bf16[8,72,1,1440]{3,0,2,1:T(8,128)(2,1)S(1)}, bf16[8,72,1,1440]{3,0,2,1:T(8,128)(2,1)}, u32[]{:S(2)}) copy-start(bf16[8,72,1,1440]{3,0,2,1:T(8,128)(2,1)} %copy-done) | copy-start | bytes 4976644
  162.4 5.6 %copy-start.2 = (f32[18,1440]{1,0:T(8,128)S(1)}, f32[18,1440]{1,0:T(8,128)}, u32[]{:S(2)}) copy-start(f32[18,1440]{1,0:T(8,128)} %bitcast_convert_fusion) | copy-start | bytes 311044
  173.8 78.8 %all-to-all-start.1 = ((bf16[32,18,1,1440]{3,1,2,0:T(8,128)(2,1)}), bf16[32,18,1,1440]{3,1,2,0:T(8,128)(2,1)}, u32[]{:S(2)}, u32[]{:S(2)}) async-start(bf16[32,18,1,1440]{3,1,2,0:T(8,128)(2,1)} %copy.47), calls=%async_computation.1 | async-start | bytes 4718592 | tf_op jit(solution)/shard_map/all_to_all | solution.py:42
where the time goes:
time: 259 us; the launch traced here: 258 us
  other arithmetic  73.8 us (28%)
  blocking collectives  69.2 us (27%)
  local copies, waits for them, and re-layouts  61.6 us (24%)
  waiting for transfers between devices  38.9 us (15%)
  starting transfers between devices  10.8 us (4%)
  between operations  3.13 us (1%)
    psum x1, blocking collectives, on_device(): total = lax.psum(partial_value, ('mem', 'lat'))  69.2 us
    reduce_sum x16, other arithmetic, one_group(): return (jnp.sum(jnp.abs(diff), axis=1), jnp.sum(jnp.sign(diff), axis=1))  58.2 us
    all_to_all x1, waiting for transfers between devices, on_device(): lax.all_to_all(ensemble, 'mem', split_axis=1, concat_axis=0, tiled=True)  38.9 us
    dynamic_update_slice x16, local copies, waits for them, and re-layouts, pair_terms(): spread, count = lax.map(one_group, grouped)  18 us
    dynamic_slice x32, local copies, waits for them, and re-layouts, pair_terms(): spread, count = lax.map(one_group, grouped)  17.2 us
    div x2, local copies, waits for them, and re-layouts, finish(): count / (members - 1)  9.32 us
    all_to_all x1, starting transfers between devices, on_device(): lax.all_to_all(ensemble, 'mem', split_axis=1, concat_axis=0, tiled=True)  6.35 us
    unnamed x8, local copies, waits for them, and re-layouts  6.13 us
  transfers between devices with their start and end apart: 2, of which 1 were waited for; matrix products, arithmetic and copies ran while one was open for 2% of the time, Pallas kernels for 0%

commit v1 on v0

v1 whole, which is shorter than its diff:
```python
import functools

import jax
import jax.numpy as jnp
from jax import lax
from jax.experimental import pallas as pl
from jax.experimental.pallas import tpu as pltpu
from jax.sharding import PartitionSpec as P

LANES = 128
ROWS = 16
TILE = 8


def cdiv(a, b):
    return -(-a // b)


class Plan:
    def __init__(self, channels, cells, groups):
        self.channels, self.cells, self.groups = channels, cells, groups
        self.bands = channels // (ROWS * groups)
        self.cols = cells // LANES
        self.body_rows = self.bands * ROWS * groups
        self.tail = cells - self.cols * LANES
        self.left_tiles = (channels - self.body_rows) // TILE
        self.body = self.bands * self.cols
        self.row_tiles = channels // TILE
        self.per_tile = LANES // self.tail if self.tail else 1
        self.tail_tiles = cdiv(self.row_tiles, self.per_tile) if self.tail else 0
        tiles = self.left_tiles * self.cols + self.tail_tiles
        self.extra = cdiv(tiles, 2 * groups)
        self.tiles = tiles
        self.blocks = self.body + self.extra
        assert channels % TILE == 0 and (self.tail == 0 or LANES % self.tail == 0)


def partner(me, b, groups):
    return lax.bitwise_xor(me, b)


def pairs_of(b, size):
    return [(i, i ^ b) for i in range(size)]


def body_slices(plan, piece, block):
    band, col = divmod(block, plan.cols)
    row = pl.multiple_of((piece * plan.bands + band) * ROWS, ROWS)
    return pl.ds(row, ROWS), pl.ds(col * LANES, LANES)


def take_body(plan, first, count, ens, truth, outs, t_out, sem):
    me = lax.axis_index("mem")
    copies = []
    for b in range(plan.groups):
        piece = partner(me, b, plan.groups)
        for i in range(count):
            rows, cols = body_slices(plan, piece, first + i)
            copies.append(
                pltpu.make_async_copy(
                    ens.at[:, rows, cols], outs[b].at[:, pl.ds(i * ROWS, ROWS), :], sem.at[len(copies)]
                )
            )
    for i in range(count):
        rows, cols = body_slices(plan, me, first + i)
        copies.append(
            pltpu.make_async_copy(truth.at[rows, cols], t_out.at[pl.ds(i * ROWS, ROWS), :], sem.at[len(copies)])
        )
    for c in copies:
        c.start()
    return copies


def pack_body_kernel(plan, first, count, ens, truth, *refs):
    outs, t_out, sem = refs[: plan.groups], refs[plan.groups], refs[plan.groups + 1]
    for c in take_body(plan, first, count, ens, truth, outs, t_out, sem):
        c.wait()


def gather_extra(plan, edge, low, extra, lead):
    pad = plan.extra * ROWS * plan.groups - plan.tiles * TILE
    if pad:
        extra[lead + (pl.ds(plan.tiles * TILE, pad), slice(None))] = jnp.zeros((pad, LANES), jnp.bfloat16)
    at = 0
    for r in range(plan.left_tiles):
        for c in range(plan.cols):
            extra[lead + (pl.ds(at * TILE, TILE), slice(None))] = low[
                lead + (pl.ds(r * TILE, TILE), pl.ds(c * LANES, LANES))
            ]
            at += 1
    lane = lax.broadcasted_iota(jnp.int32, (TILE, LANES), 1)
    for t in range(plan.tail_tiles):
        value = jnp.zeros((TILE, LANES), jnp.float32)
        for i in range(plan.per_tile):
            r = t * plan.per_tile + i
            if r < plan.row_tiles:
                one = edge[lead + (pl.ds(r * TILE, TILE), slice(None))].astype(jnp.float32)
                if i:
                    one = pltpu.roll(one, i * plan.tail, 1)
                inside = (lane >= i * plan.tail) & (lane < (i + 1) * plan.tail)
                value = jnp.where(inside, one, value)
        extra[lead + (pl.ds(at * TILE, TILE), slice(None))] = value.astype(jnp.bfloat16)
        at += 1


def pack_rest_kernel(plan, first, count, ens, truth, ens_edge, ens_low, t_edge, t_low, *refs):
    n = plan.groups
    outs, t_out, sem, extra, t_extra = refs[:n], refs[n], refs[n + 1], refs[n + 2], refs[n + 3]
    copies = take_body(plan, first, count, ens, truth, outs, t_out, sem)
    me = lax.axis_index("mem")
    rows = plan.extra * ROWS
    members = ens.shape[0]
    for m in range(members):
        gather_extra(plan, ens_edge, ens_low, extra, (m,))
    gather_extra(plan, t_edge, t_low, t_extra, ())
    for b in range(n):
        at = pl.multiple_of(partner(me, b, n) * rows, ROWS)
        for m in range(members):
            outs[b][m, pl.ds(count * ROWS, rows), :] = extra[m, pl.ds(at, rows), :]
    t_out[pl.ds(count * ROWS, rows), :] = t_extra[pl.ds(pl.multiple_of(me * rows, ROWS), rows), :]
    for c in copies:
        c.wait()


VMEM = pl.BlockSpec(memory_space=pltpu.VMEM)
ANY = pl.BlockSpec(memory_space=pl.ANY)


def pack(plan, ens, truth, first, count, with_extra):
    members = ens.shape[0]
    rows = (count + (plan.extra if with_extra else 0)) * ROWS
    n = plan.groups
    shapes = [jax.ShapeDtypeStruct((members, rows, LANES), jnp.bfloat16)] * n
    shapes.append(jax.ShapeDtypeStruct((rows, LANES), jnp.bfloat16))
    sems = pltpu.SemaphoreType.DMA(((n + 1) * count,))
    if not with_extra:
        return pl.pallas_call(
            functools.partial(pack_body_kernel, plan, first, count),
            out_shape=shapes,
            in_specs=[ANY, ANY],
            out_specs=[VMEM] * (n + 1),
            scratch_shapes=[sems],
            name="pack_body",
        )(ens, truth)
    low = (plan.channels - plan.body_rows)
    specs = [
        ANY,
        ANY,
        pl.BlockSpec((members, plan.channels, LANES), lambda i: (0, 0, plan.cols)),
        pl.BlockSpec((members, low, plan.cells), lambda i: (0, plan.body_rows // low, 0)),
        pl.BlockSpec((plan.channels, LANES), lambda i: (0, plan.cols)),
        pl.BlockSpec((low, plan.cells), lambda i: (plan.body_rows // low, 0)),
    ]
    all_rows = plan.extra * ROWS * n
    return pl.pallas_call(
        functools.partial(pack_rest_kernel, plan, first, count),
        grid=(1,),
        out_shape=shapes,
        in_specs=specs,
        out_specs=[pl.BlockSpec(s.shape, lambda i, k=len(s.shape): (0,) * k) for s in shapes],
        scratch_shapes=[
            sems,
            pltpu.VMEM((members, all_rows, LANES), jnp.bfloat16),
            pltpu.VMEM((all_rows, LANES), jnp.bfloat16),
        ],
        name="pack_rest",
    )(ens, truth, ens, ens, truth, truth)


def sign_of(diff):
    big = jnp.asarray(2.0**127, jnp.bfloat16)
    one = jnp.asarray(1.0, jnp.bfloat16)
    return jnp.minimum(jnp.maximum(diff * big, -one), one)


def count_kernel(n, members, blocks, scale, weight, t_ref, *refs):
    vals, before, grads, loss, counts = refs[:n], refs[n], refs[n + 1 : 2 * n + 1], refs[2 * n + 1], refs[2 * n + 2]
    local = members // n
    w = weight[0]
    step = w / (members - 1.0)

    def block(i, total):
        rows = pl.ds(pl.multiple_of(i * ROWS, ROWS), ROWS)

        def load(g):
            return [vals[g][m, rows, :] for m in range(local)]

        for a in range(n):
            ea = load(a)
            ca = [counts[a * local + m] if a else None for m in range(local)]

            def bump(old, s, up):
                if old is None:
                    return s if up else -s
                return old + s if up else old - s

            for k in range(local):
                for j in range(k + 1, local):
                    s = sign_of(ea[k] - ea[j])
                    ca[k] = bump(ca[k], s, True)
                    ca[j] = bump(ca[j], s, False)
            for b in range(a + 1, n):
                eb = load(b)
                for j in range(local):
                    cj = counts[b * local + j] if a else None
                    for k in range(local):
                        s = sign_of(ea[k] - eb[j])
                        ca[k] = bump(ca[k], s, True)
                        cj = bump(cj, s, False)
                    counts[b * local + j] = cj
            t = t_ref[rows, :]
            t32 = t.astype(jnp.float32)
            most = jnp.asarray(members - 1.0, jnp.bfloat16)
            for k in range(local):
                num = (most * sign_of(ea[k] - t) - ca[k]).astype(jnp.float32)
                grads[a][k, rows, :] = (num * step).astype(jnp.bfloat16)
                total = total + (ea[k].astype(jnp.float32) - t32) * num
        return total

    total = lax.fori_loop(0, blocks, block, jnp.zeros((ROWS, LANES), jnp.float32))
    loss[...] = before[...] + jnp.sum(total) * (w * scale)


def count_terms(values, target, weight, before, scale, members):
    n = len(values)
    local, rows, _ = values[0].shape
    blocks = rows // ROWS
    return pl.pallas_call(
        functools.partial(count_kernel, n, members, blocks, scale),
        out_shape=[jax.ShapeDtypeStruct(v.shape, jnp.bfloat16) for v in values]
        + [jax.ShapeDtypeStruct((TILE, LANES), jnp.float32)],
        in_specs=[pl.BlockSpec(memory_space=pltpu.SMEM)] + [VMEM] * (n + 2),
        out_specs=[VMEM] * (n + 1),
        scratch_shapes=[pltpu.VMEM((members, ROWS, LANES), jnp.bfloat16)],
        cost_estimate=pl.CostEstimate(
            flops=members * members * 3 * rows * LANES, bytes_accessed=4 * n * local * rows * LANES, transcendentals=0
        ),
        name="count",
    )(weight, target, *values, before)


def spread_extra(plan, extra, edge, lead):
    at = plan.left_tiles * plan.cols
    for t in range(plan.tail_tiles):
        value = extra[lead + (pl.ds((at + t) * TILE, TILE), slice(None))].astype(jnp.float32)
        for i in range(plan.per_tile):
            r = t * plan.per_tile + i
            if r < plan.row_tiles:
                one = pltpu.roll(value, LANES - i * plan.tail, 1) if i else value
                edge[lead + (pl.ds(r * TILE, TILE), slice(None))] = one.astype(jnp.bfloat16)


def edge_kernel(plan, count, *refs):
    n = plan.groups
    ins, out, extra = refs[:n], refs[n], refs[n + 1]
    me = lax.axis_index("mem")
    rows = plan.extra * ROWS
    members = ins[0].shape[0]
    for b in range(n):
        at = pl.multiple_of(partner(me, b, n) * rows, ROWS)
        for m in range(members):
            extra[m, pl.ds(at, rows), :] = ins[b][m, pl.ds(count * ROWS, rows), :]
    for m in range(members):
        spread_extra(plan, extra, out, (m,))


def write_edge(plan, pieces, count):
    members = pieces[0].shape[0]
    n = plan.groups
    full = lambda s: pl.BlockSpec(s, lambda i, k=len(s): (0,) * k)
    all_rows = plan.extra * ROWS * n
    return pl.pallas_call(
        functools.partial(edge_kernel, plan, count),
        grid=(1,),
        out_shape=jax.ShapeDtypeStruct((members, plan.channels, plan.cells), jnp.bfloat16),
        in_specs=[full(p.shape) for p in pieces],
        out_specs=pl.BlockSpec((members, plan.channels, LANES), lambda i: (0, 0, plan.cols)),
        scratch_shapes=[pltpu.VMEM((members, all_rows, LANES), jnp.bfloat16)],
        name="write_edge",
    )(*pieces)


def put_kernel(plan, first, count, with_extra, which, *refs):
    n = len(which)
    ins, out, sem = refs[1 : n + 1], refs[n + 1], refs[n + 2]
    me = lax.axis_index("mem")
    copies = []
    for p, b in enumerate(which):
        piece = partner(me, b, plan.groups)
        for i in range(count):
            rows, cols = body_slices(plan, piece, first + i)
            copies.append(
                pltpu.make_async_copy(
                    ins[p].at[:, pl.ds(i * ROWS, ROWS), :], out.at[:, rows, cols], sem.at[len(copies)]
                )
            )
    for c in copies:
        c.start()
    if with_extra:
        per = 2 * plan.extra
        total = plan.left_tiles * plan.cols
        for p, b in enumerate(which):
            piece = partner(me, b, plan.groups)
            for i in range(per):
                tile = piece * per + i

                def one(p=p, i=i, tile=tile):
                    row = pl.multiple_of(plan.body_rows + tile // plan.cols * TILE, TILE)
                    col = pl.multiple_of(lax.rem(tile, plan.cols) * LANES, LANES)
                    c = pltpu.make_async_copy(
                        ins[p].at[:, pl.ds(count * ROWS + i * TILE, TILE), :],
                        out.at[:, pl.ds(row, TILE), pl.ds(col, LANES)],
                        sem.at[n * count + p * per + i],
                    )
                    c.start()
                    c.wait()

                pl.when(tile < total)(one)
    for c in copies:
        c.wait()


def put(plan, out, pieces, first, count, with_extra, which):
    n = len(pieces)
    return pl.pallas_call(
        functools.partial(put_kernel, plan, first, count, with_extra, which),
        out_shape=jax.ShapeDtypeStruct(out.shape, out.dtype),
        in_specs=[ANY] + [VMEM] * n,
        out_specs=ANY,
        scratch_shapes=[pltpu.SemaphoreType.DMA((n * (count + 2 * plan.extra),))],
        input_output_aliases={0: 0},
        name="put",
    )(out, *pieces)


def exchange(pieces, groups):
    out = [pieces[0]] + [None] * (groups - 1)
    for b in reversed(range(1, groups)):
        out[b] = lax.ppermute(pieces[b], "mem", pairs_of(b, groups))
    return out


def butterfly(value, axis, size):
    step = 1
    while step < size:
        value = value + lax.ppermute(value, axis, pairs_of(step, size))
        step *= 2
    return value


def on_device(groups, lats, ensemble, truth, row_weight):
    local, channels, rows, cells = ensemble.shape
    members = local * groups
    plan = Plan(channels, cells, groups)
    ens = ensemble.reshape(local, channels, cells)
    tru = truth.reshape(channels, cells)
    scale = 1.0 / (members * (members - 1.0)) / (channels * rows * lats * cells)
    first = plan.body // 2
    rest = plan.body - first

    a = pack(plan, ens, tru, 0, first, False)
    a_in = exchange(a[:groups], groups)
    c = pack(plan, ens, tru, first, rest, True)
    c_in = exchange(c[:groups], groups)

    zero = jnp.zeros((TILE, LANES), jnp.float32)
    *a_grad, part = count_terms(a_in, a[groups], row_weight, zero, scale, members)
    a_out = exchange(a_grad, groups)
    *c_grad, part = count_terms(c_in, c[groups], row_weight, part, scale, members)
    part = butterfly(part, "lat", lats)
    part = butterfly(part, "mem", groups)
    c_out = exchange(c_grad, groups)

    every = tuple(range(groups))
    out = write_edge(plan, c_out, rest)
    out = put(plan, out, a_out, 0, first, False, every)
    out = put(plan, out, c_out, first, rest, True, every)
    return part[0, 0], out.reshape(ensemble.shape)


def solution(mesh):
    placed = (P("mem", None, "lat", None), P(None, "lat", None), P("lat"))
    return jax.shard_map(
        functools.partial(on_device, mesh.shape["mem"], mesh.shape["lat"]),
        mesh=mesh,
        in_specs=placed,
        out_specs=(P(), P("mem", None, "lat", None)),
        check_vma=False,
    )
```

time: 259 us -> 115 us (0.44)
  other arithmetic: 73.8 us -> 0.69 us
  blocking collectives: 69.2 us -> 0 us
  local copies, waits for them, and re-layouts: 61.6 us -> 3.58 us
  Pallas kernels: 0 us -> 32.1 us
  starting transfers between devices: 10.8 us -> 29.2 us
  waiting for transfers between devices: 38.9 us -> 47.7 us
    psum x1 -> x0, blocking collectives: 69.2 us -> none  [on_device(): total = lax.psum(partial_value, ('mem', 'lat'))]
    reduce_sum x19 -> x0, other arithmetic: 62.6 us -> none  [the longest x16 58.2 us: one_group(): return (jnp.sum(jnp.abs(diff), axis=1), jnp.sum(jnp.sign(diff), axis=1))]
    ppermute x0 -> x17, waiting for transfers between devices: none -> 47.7 us  [the longest x12 34.6 us: exchange(): out[b] = lax.ppermute(pieces[b], 'mem', pairs_of(b, groups))]
    all_to_all x2 -> x0, waiting for transfers between devices: 38.9 us -> none  [the longest x1 38.9 us: on_device(): lax.all_to_all(ensemble, 'mem', split_axis=1, concat_axis=0, tiled=True)]
    pallas_call x0 -> x7, Pallas kernels: none -> 32.1 us  [the longest x2 13.8 us: count_terms(): pl.pallas_call(functools.partial(count_kernel, n, members, blocks, scale)...]
    ppermute x0 -> x17, starting transfers between devices: none -> 29.2 us  [the longest x12 21.7 us: exchange(): out[b] = lax.ppermute(pieces[b], 'mem', pairs_of(b, groups))]
    dynamic_update_slice x16 -> x0, local copies, waits for them, and re-layouts: 18 us -> none  [pair_terms(): spread, count = lax.map(one_group, grouped)]
    dynamic_slice x32 -> x0, local copies, waits for them, and re-layouts: 17.2 us -> none  [pair_terms(): spread, count = lax.map(one_group, grouped)]
  transfers between devices with their start and end apart: 2 -> 17, of which waited for: 1 -> 7; matrix products, arithmetic and copies ran while one was open for 2% -> 2% of each run, Pallas kernels for 0% -> 10%
where the time goes in v1:
time: 115 us
  waiting for transfers between devices  47.7 us (41%)
  Pallas kernels  32.1 us (28%)
  starting transfers between devices  29.2 us (25%)
  local copies, waits for them, and re-layouts  3.58 us (3%)
  between operations  1.41 us (1%)
    ppermute x12, waiting for transfers between devices, exchange(): out[b] = lax.ppermute(pieces[b], 'mem', pairs_of(b, groups))  34.6 us
    ppermute x12, starting transfers between devices, exchange(): out[b] = lax.ppermute(pieces[b], 'mem', pairs_of(b, groups))  21.7 us
    pallas_call x2, Pallas kernels, count_terms(): pl.pallas_call(functools.partial(count_kernel, n, members, blocks, scale)...  13.8 us
    ppermute x5, waiting for transfers between devices, butterfly(): value = value + lax.ppermute(value, axis, pairs_of(step, size))  13.1 us
    pallas_call x2, Pallas kernels, put(): pl.pallas_call(functools.partial(put_kernel, plan, first, count, with_ext...  10.8 us
    ppermute x5, starting transfers between devices, butterfly(): value = value + lax.ppermute(value, axis, pairs_of(step, size))  7.48 us
    pallas_call x1, Pallas kernels, pack(): pl.pallas_call(functools.partial(pack_rest_kernel, plan, first, count), g...  3.37 us
    unnamed x28, local copies, waits for them, and re-layouts  2.46 us
  transfers between devices with their start and end apart: 17, of which 7 were waited for; matrix products, arithmetic and copies ran while one was open for 2% of the time, Pallas kernels for 10%

profile of v1, /device:TPU:0, one launch (start us, length us, event | category | flops | bytes accessed | tf_op | source)
XLA Modules:
  0.0 114.6 jit_solution(18186382214266969117)
XLA Ops:
  0.6 2.2 %pack_body.1 = (bf16[8,80,128]{2,1,0:T(8,128)(2,1)}, bf16[8,80,128]{2,1,0:T(8,128)(2,1)}, bf16[8,80,128]{2,1,0:T(8,128)(2,1)}, bf16[8,80,128]{2,1,0:T(8,128)(2,1)}, bf16[80,128]{1,0:T(8,128)(2,1)}) custom-call(bf16[8,72,1440]{2,1,0:T(8,128)(2,1)} %bitcast.6, bf16[72,1440]{1,0:T(8,128)(2,1)} %bitcast.11), custom_call_target="tpu_custom_call" | custom-call | tf_op jit(solution)/shard_map/pack_body/pallas_call | solution.py:137
  2.9 0.0 copy-start.13
  2.9 0.0 copy-start.12
  2.9 3.1 %collective-permute-start.3 = (bf16[8,80,128]{2,1,0:T(8,128)(2,1)}, bf16[8,80,128]{2,1,0:T(8,128)(2,1)S(1)}, u32[]{:S(2)}, u32[]{:S(2)}) collective-permute-start(bf16[8,80,128]{2,1,0:T(8,128)(2,1)} %get-tuple-element.29), channel_id=1, source_target_pairs={{0,8},{8,0},{16,24},{24,16},{1,9},{9,1},{17,25},{25,17},{2,10},{10... | collective-permute-start | bytes 491528 | tf_op jit(solution)/shard_map/ppermute | solution.py:339
  6.0 3.4 %pack_rest.1 = (bf16[8,128,128]{2,1,0:T(8,128)(2,1)}, bf16[8,128,128]{2,1,0:T(8,128)(2,1)}, bf16[8,128,128]{2,1,0:T(8,128)(2,1)}, bf16[8,128,128]{2,1,0:T(8,128)(2,1)}, bf16[128,128]{1,0:T(8,128)(2,1)}) custom-call(bf16[8,72,1440]{2,1,0:T(8,128)(2,1)} %bitcast.7, bf16[72,1440]{1,0:T(8,128)(2,1)} %bitcast.12, bf16[8,72,1440]{2,1,0:T(8,128)(2,1)} %bitcast.8, ...), custom_call_target="tpu_custom_call" | custom-call | tf_op jit(solution)/shard_map/pack_rest/pallas_call | solution.py:155
  9.4 0.1 collective-permute-start
  9.5 3.0 %collective-permute-start.1 = (bf16[8,128,128]{2,1,0:T(8,128)(2,1)}, bf16[8,128,128]{2,1,0:T(8,128)(2,1)S(1)}, u32[]{:S(2)}, u32[]{:S(2)}) collective-permute-start(bf16[8,128,128]{2,1,0:T(8,128)(2,1)} %get-tuple-element.25), channel_id=1, source_target_pairs={{0,16},{8,24},{16,0},{24,8},{1,17},{9,25},{17,1},{25,9},{2,18},{10... | collective-permute-start | bytes 786440 | tf_op jit(solution)/shard_map/ppermute | solution.py:339
  12.5 1.3 %collective-permute-start.2 = (bf16[8,128,128]{2,1,0:T(8,128)(2,1)}, bf16[8,128,128]{2,1,0:T(8,128)(2,1)S(1)}, u32[]{:S(2)}, u32[]{:S(2)}) collective-permute-start(bf16[8,128,128]{2,1,0:T(8,128)(2,1)} %get-tuple-element.26), channel_id=1, source_target_pairs={{0,24},{8,16},{16,8},{24,0},{1,25},{9,17},{17,9},{25,1},{2,26},{10... | collective-permute-start | bytes 786440 | tf_op jit(solution)/shard_map/ppermute | solution.py:339
  13.8 0.0 copy-done.13
  13.8 1.7 %collective-permute-start.4 = (bf16[8,80,128]{2,1,0:T(8,128)(2,1)S(1)}, bf16[8,80,128]{2,1,0:T(8,128)(2,1)S(1)}, u32[]{:S(2)}, u32[]{:S(2)}) collective-permute-start(bf16[8,80,128]{2,1,0:T(8,128)(2,1)S(1)} %copy-done.13), channel_id=1, source_target_pairs={{0,16},{8,24},{16,0},{24,8},{1,17},{9,25},{17,1},{25,9},{2,18},{10... | collective-permute-start | bytes 491528 | tf_op jit(solution)/shard_map/ppermute | solution.py:339
  15.5 0.0 collective-permute-done.3.refs_1_
  15.5 0.0 copy-start.9
  15.5 0.0 copy-done.12
  15.5 1.0 collective-permute-start.5
  17.1 30.1 %collective-permute-done.4.refs_2_ = bf16[8,80,128]{2,1,0:T(8,128)(2,1)S(1)} collective-permute-done((bf16[8,80,128]{2,1,0:T(8,128)(2,1)S(1)}, bf16[8,80,128]{2,1,0:T(8,128)(2,1)S(1)}, u32[]{:S(2)}, u32[]{:S(2)}) %collective-permute-start.4) | collective-permute-done | bytes 163872 | tf_op jit(solution)/shard_map/ppermute | solution.py:339
  47.2 0.0 collective-permute-done.5.refs_3_
  47.2 0.6 broadcast_in_dim.3.refs_4_
  47.8 0.0 copy-done.9
  47.8 0.1 copy-done.10
  47.9 0.1 copy-done.11
  48.0 5.7 %count.2 = (bf16[8,80,128]{2,1,0:T(8,128)(2,1)}, bf16[8,80,128]{2,1,0:T(8,128)(2,1)}, bf16[8,80,128]{2,1,0:T(8,128)(2,1)}, bf16[8,80,128]{2,1,0:T(8,128)(2,1)}, f32[8,128]{1,0:T(8,128)}) custom-call(f32[1]{0:T(128)S(6)} %copy.10.weight, bf16[80,128]{1,0:T(8,128)(2,1)} %get-tuple-element.27.t_ref, bf16[8,80,128]{2,1,0:T(8,128)(2,1)} %get-tuple-element.28.refs_0_, ...), custom_call_target="tpu_custom_call" | custom-call | flops 31457280 | bytes 1310720 | tf_op jit(solution)/shard_map/count/pallas_call | solution.py:228
  53.7 0.0 collective-permute-done.refs_1_
  53.7 0.0 collective-permute-done.1.refs_2_
  53.7 0.0 copy-start.4
  53.7 0.0 collective-permute-done.2.refs_3_
  53.7 0.0 copy-start.5
  53.7 0.7 copy-done.3
  54.4 0.1 copy-done.4
  54.5 0.1 copy-done.5
  54.5 8.1 %count.3 = (bf16[8,128,128]{2,1,0:T(8,128)(2,1)}, bf16[8,128,128]{2,1,0:T(8,128)(2,1)}, bf16[8,128,128]{2,1,0:T(8,128)(2,1)}, bf16[8,128,128]{2,1,0:T(8,128)(2,1)}, f32[8,128]{1,0:T(8,128)}) custom-call(f32[1]{0:T(128)S(6)} %copy.10.weight, bf16[128,128]{1,0:T(8,128)(2,1)} %get-tuple-element.22.t_ref, bf16[8,128,128]{2,1,0:T(8,128)(2,1)} %get-tuple-element.23.refs_0_, ...), custom_call_target="tpu_custom_call" | custom-call | flops 50331648 | bytes 2097152 | tf_op jit(solution)/shard_map/count/pallas_call | solution.py:228
  62.6 2.9 %collective-permute-start.11 = (bf16[8,128,128]{2,1,0:T(8,128)(2,1)}, bf16[8,128,128]{2,1,0:T(8,128)(2,1)S(1)}, u32[]{:S(2)}, u32[]{:S(2)}) collective-permute-start(bf16[8,128,128]{2,1,0:T(8,128)(2,1)} %get-tuple-element.35), channel_id=1, source_target_pairs={{0,8},{8,0},{16,24},{24,16},{1,9},{9,1},{17,25},{25,17},{2,10},{10... | collective-permute-start | bytes 786440 | tf_op jit(solution)/shard_map/ppermute | solution.py:339
  65.5 1.9 %collective-permute-start.12 = (bf16[8,128,128]{2,1,0:T(8,128)(2,1)}, bf16[8,128,128]{2,1,0:T(8,128)(2,1)S(1)}, u32[]{:S(2)}, u32[]{:S(2)}) collective-permute-start(bf16[8,128,128]{2,1,0:T(8,128)(2,1)} %get-tuple-element.36), channel_id=1, source_target_pairs={{0,16},{8,24},{16,0},{24,8},{1,17},{9,25},{17,1},{25,9},{2,18},{10... | collective-permute-start | bytes 786440 | tf_op jit(solution)/shard_map/ppermute | solution.py:339
  67.5 1.5 %collective-permute-start.13 = (bf16[8,128,128]{2,1,0:T(8,128)(2,1)}, bf16[8,128,128]{2,1,0:T(8,128)(2,1)S(1)}, u32[]{:S(2)}, u32[]{:S(2)}) collective-permute-start(bf16[8,128,128]{2,1,0:T(8,128)(2,1)} %get-tuple-element.37), channel_id=1, source_target_pairs={{0,24},{8,16},{16,8},{24,0},{1,25},{9,17},{17,9},{25,1},{2,26},{10... | collective-permute-start | bytes 786440 | tf_op jit(solution)/shard_map/ppermute | solution.py:339
  68.9 0.0 collective-permute-start.6
  68.9 1.4 %collective-permute-done.6 = f32[8,128]{1,0:T(8,128)S(1)} collective-permute-done((f32[8,128]{1,0:T(8,128)}, f32[8,128]{1,0:T(8,128)S(1)}, u32[]{:S(2)}, u32[]{:S(2)}) %collective-permute-start.6) | collective-permute-done | bytes 4128 | tf_op jit(solution)/shard_map/ppermute | solution.py:346
  70.3 0.7 add.15
  71.0 1.5 %collective-permute-start.7 = (f32[8,128]{1,0:T(8,128)S(1)}, f32[8,128]{1,0:T(8,128)S(1)}, u32[]{:S(2)}, u32[]{:S(2)}) collective-permute-start(f32[8,128]{1,0:T(8,128)S(1)} %add.15), channel_id=1, source_target_pairs={{0,2},{1,3},{2,0},{3,1},{4,6},{5,7},{6,4},{7,5},{8,10},{9,11},{10,... | collective-permute-start | bytes 12296 | tf_op jit(solution)/shard_map/ppermute | solution.py:346
  72.5 2.1 %collective-permute-done.7 = f32[8,128]{1,0:T(8,128)S(1)} collective-permute-done((f32[8,128]{1,0:T(8,128)S(1)}, f32[8,128]{1,0:T(8,128)S(1)}, u32[]{:S(2)}, u32[]{:S(2)}) %collective-permute-start.7) | collective-permute-done | bytes 4128 | tf_op jit(solution)/shard_map/ppermute | solution.py:346
  74.6 1.5 %collective-permute-start.8 = (f32[8,128]{1,0:T(8,128)S(1)}, f32[8,128]{1,0:T(8,128)S(1)}, u32[]{:S(2)}, u32[]{:S(2)}) collective-permute-start(f32[8,128]{1,0:T(8,128)S(1)} %add.16), channel_id=1, source_target_pairs={{0,4},{1,5},{2,6},{3,7},{4,0},{5,1},{6,2},{7,3},{8,12},{9,13},{10,... | collective-permute-start | bytes 12296 | tf_op jit(solution)/shard_map/ppermute | solution.py:346
  76.1 2.1 %collective-permute-done.8 = f32[8,128]{1,0:T(8,128)S(1)} collective-permute-done((f32[8,128]{1,0:T(8,128)S(1)}, f32[8,128]{1,0:T(8,128)S(1)}, u32[]{:S(2)}, u32[]{:S(2)}) %collective-permute-start.8) | collective-permute-done | bytes 4128 | tf_op jit(solution)/shard_map/ppermute | solution.py:346
  78.2 0.6 collective-permute-start.9
  78.8 3.1 %collective-permute-done.9 = f32[8,128]{1,0:T(8,128)S(1)} collective-permute-done((f32[8,128]{1,0:T(8,128)S(1)}, f32[8,128]{1,0:T(8,128)S(1)}, u32[]{:S(2)}, u32[]{:S(2)}) %collective-permute-start.9) | collective-permute-done | bytes 4128 | tf_op jit(solution)/shard_map/ppermute | solution.py:346
  81.9 3.9 %collective-permute-start.10 = (f32[8,128]{1,0:T(8,128)S(1)}, f32[8,128]{1,0:T(8,128)S(1)}, u32[]{:S(2)}, u32[]{:S(2)}) collective-permute-start(f32[8,128]{1,0:T(8,128)S(1)} %add.18), channel_id=1, source_target_pairs={{0,16},{8,24},{16,0},{24,8},{1,17},{9,25},{17,1},{25,9},{2,18},{10... | collective-permute-start | bytes 12296 | tf_op jit(solution)/shard_map/ppermute | solution.py:346
  85.8 0.0 collective-permute-start.14
  85.8 4.5 %collective-permute-done.10 = f32[8,128]{1,0:T(8,128)S(1)} collective-permute-done((f32[8,128]{1,0:T(8,128)S(1)}, f32[8,128]{1,0:T(8,128)S(1)}, u32[]{:S(2)}, u32[]{:S(2)}) %collective-permute-start.10) | collective-permute-done | bytes 4128 | tf_op jit(solution)/shard_map/ppermute | solution.py:346
  90.2 0.1 collective-permute-start.15
  90.4 0.0 collective-permute-done.11.refs_1_.refs_2_
  90.4 5.0 %collective-permute-start.16 = (bf16[8,80,128]{2,1,0:T(8,128)(2,1)}, bf16[8,80,128]{2,1,0:T(8,128)(2,1)S(1)}, u32[]{:S(2)}, u32[]{:S(2)}) collective-permute-start(bf16[8,80,128]{2,1,0:T(8,128)(2,1)} %get-tuple-element.41), channel_id=1, source_target_pairs={{0,24},{8,16},{16,8},{24,0},{1,25},{9,17},{17,9},{25,1},{2,26},{10... | collective-permute-start | bytes 491528 | tf_op jit(solution)/shard_map/ppermute | solution.py:339
  95.4 0.5 slice.3
  95.9 0.0 collective-permute-done.12.refs_2_.refs_3_
  95.9 0.0 collective-permute-done.13.refs_3_.refs_4_
  95.9 0.0 copy-start.2
  95.9 0.0 copy-done
  95.9 0.7 copy-done.1
  96.6 0.1 copy-done.2
  96.7 2.0 %write_edge.1.refs_0_ = bf16[8,72,1440]{2,1,0:T(8,128)(2,1)} custom-call(bf16[8,128,128]{2,1,0:T(8,128)(2,1)} %get-tuple-element.34.refs_0_.refs_1_, bf16[8,128,128]{2,1,0:T(8,128)(2,1)} %copy-done, bf16[8,128,128]{2,1,0:T(8,128)(2,1)} %copy-done.1, bf16[8,128,128]{2,1,0:T(8,128)(2,1)} %copy-done.2), custom_call_target="tpu_custom_call" | custom-call | tf_op jit(solution)/shard_map/write_edge/pallas_call | solution.py:272
  98.7 0.0 collective-permute-done.14.refs_2_
  98.7 4.4 %collective-permute-done.15.refs_3_ = bf16[8,80,128]{2,1,0:T(8,128)(2,1)S(1)} collective-permute-done((bf16[8,80,128]{2,1,0:T(8,128)(2,1)}, bf16[8,80,128]{2,1,0:T(8,128)(2,1)S(1)}, u32[]{:S(2)}, u32[]{:S(2)}) %collective-permute-start.15) | collective-permute-done | bytes 163872 | tf_op jit(solution)/shard_map/ppermute | solution.py:339
  103.1 0.0 collective-permute-done.16.refs_4_
  103.1 0.0 copy-done.6
  103.1 0.6 copy-done.7
  103.8 0.1 copy-done.8
  103.8 2.3 %put.2.refs_0_ = bf16[8,72,1440]{2,1,0:T(8,128)(2,1)} custom-call(bf16[8,72,1440]{2,1,0:T(8,128)(2,1)} %write_edge.1.refs_0_, bf16[8,80,128]{2,1,0:T(8,128)(2,1)} %get-tuple-element.38.refs_1_, bf16[8,80,128]{2,1,0:T(8,128)(2,1)} %copy-done.6, bf16[8,80,128]{2,1,0:T(8,128)(2,1)} %copy-done.7, ...), custom_call_target="tpu_custom_call", output_to_operand_aliasing={{}: (0, {})} | custom-call | tf_op jit(solution)/shard_map/put/pallas_call | solution.py:325
  106.1 8.5 %put.3 = bf16[8,72,1440]{2,1,0:T(8,128)(2,1)} custom-call(bf16[8,72,1440]{2,1,0:T(8,128)(2,1)} %put.2.refs_0_, bf16[8,128,128]{2,1,0:T(8,128)(2,1)} %get-tuple-element.34.refs_0_.refs_1_, bf16[8,128,128]{2,1,0:T(8,128)(2,1)} %copy-done, bf16[8,128,128]{2,1,0:T(8,128)(2,1)} %copy-done.1, bf16[8,128,128]{2,1,0:T(8,128)(2,1)} %copy-done.2), custom_call_target="tpu_custom_call", output_to_operand_aliasing={{}: (0, {})} | custom-call | tf_op jit(solution)/shard_map/put/pallas_call | solution.py:325
  (12 shorter events, 0.0 us)
Async XLA Ops:
  2.9 11.0 %copy-start.13 = (bf16[8,80,128]{2,1,0:T(8,128)(2,1)S(1)}, bf16[8,80,128]{2,1,0:T(8,128)(2,1)}, u32[]{:S(2)}) copy-start(bf16[8,80,128]{2,1,0:T(8,128)(2,1)} %get-tuple-element.30) | copy-start | bytes 491524
  2.9 12.7 %copy-start.12 = (bf16[8,80,128]{2,1,0:T(8,128)(2,1)S(1)}, bf16[8,80,128]{2,1,0:T(8,128)(2,1)}, u32[]{:S(2)}) copy-start(bf16[8,80,128]{2,1,0:T(8,128)(2,1)} %get-tuple-element.31) | copy-start | bytes 491524
  2.9 12.6 %collective-permute-start.3 = (bf16[8,80,128]{2,1,0:T(8,128)(2,1)}, bf16[8,80,128]{2,1,0:T(8,128)(2,1)S(1)}, u32[]{:S(2)}, u32[]{:S(2)}) collective-permute-start(bf16[8,80,128]{2,1,0:T(8,128)(2,1)} %get-tuple-element.29), channel_id=1, source_target_pairs={{0,8},{8,0},{16,24},{24,16},{1,9},{9,1},{17,25},{25,17},{2,10},{10... | collective-permute-start | bytes 491528 | tf_op jit(solution)/shard_map/ppermute | solution.py:339
  9.4 44.3 %collective-permute-start = (bf16[8,128,128]{2,1,0:T(8,128)(2,1)}, bf16[8,128,128]{2,1,0:T(8,128)(2,1)S(1)}, u32[]{:S(2)}, u32[]{:S(2)}) collective-permute-start(bf16[8,128,128]{2,1,0:T(8,128)(2,1)} %get-tuple-element.24), channel_id=1, source_target_pairs={{0,8},{8,0},{16,24},{24,16},{1,9},{9,1},{17,25},{25,17},{2,10},{10... | collective-permute-start | bytes 786440 | tf_op jit(solution)/shard_map/ppermute | solution.py:339
  9.5 44.2 %collective-permute-start.1 = (bf16[8,128,128]{2,1,0:T(8,128)(2,1)}, bf16[8,128,128]{2,1,0:T(8,128)(2,1)S(1)}, u32[]{:S(2)}, u32[]{:S(2)}) collective-permute-start(bf16[8,128,128]{2,1,0:T(8,128)(2,1)} %get-tuple-element.25), channel_id=1, source_target_pairs={{0,16},{8,24},{16,0},{24,8},{1,17},{9,25},{17,1},{25,9},{2,18},{10... | collective-permute-start | bytes 786440 | tf_op jit(solution)/shard_map/ppermute | solution.py:339
  12.5 41.2 %collective-permute-start.2 = (bf16[8,128,128]{2,1,0:T(8,128)(2,1)}, bf16[8,128,128]{2,1,0:T(8,128)(2,1)S(1)}, u32[]{:S(2)}, u32[]{:S(2)}) collective-permute-start(bf16[8,128,128]{2,1,0:T(8,128)(2,1)} %get-tuple-element.26), channel_id=1, source_target_pairs={{0,24},{8,16},{16,8},{24,0},{1,25},{9,17},{17,9},{25,1},{2,26},{10... | collective-permute-start | bytes 786440 | tf_op jit(solution)/shard_map/ppermute | solution.py:339
  13.8 33.4 %collective-permute-start.4 = (bf16[8,80,128]{2,1,0:T(8,128)(2,1)S(1)}, bf16[8,80,128]{2,1,0:T(8,128)(2,1)S(1)}, u32[]{:S(2)}, u32[]{:S(2)}) collective-permute-start(bf16[8,80,128]{2,1,0:T(8,128)(2,1)S(1)} %copy-done.13), channel_id=1, source_target_pairs={{0,16},{8,24},{16,0},{24,8},{1,17},{9,25},{17,1},{25,9},{2,18},{10... | collective-permute-start | bytes 491528 | tf_op jit(solution)/shard_map/ppermute | solution.py:339
  15.5 32.3 %copy-start.9 = (bf16[8,80,128]{2,1,0:T(8,128)(2,1)}, bf16[8,80,128]{2,1,0:T(8,128)(2,1)S(1)}, u32[]{:S(2)}) copy-start(bf16[8,80,128]{2,1,0:T(8,128)(2,1)S(1)} %collective-permute-done.3.refs_1_) | copy-start | bytes 491524
  15.5 31.7 %collective-permute-start.5 = (bf16[8,80,128]{2,1,0:T(8,128)(2,1)S(1)}, bf16[8,80,128]{2,1,0:T(8,128)(2,1)S(1)}, u32[]{:S(2)}, u32[]{:S(2)}) collective-permute-start(bf16[8,80,128]{2,1,0:T(8,128)(2,1)S(1)} %copy-done.12), channel_id=1, source_target_pairs={{0,24},{8,16},{16,8},{24,0},{1,25},{9,17},{17,9},{25,1},{2,26},{10... | collective-permute-start | bytes 491528 | tf_op jit(solution)/shard_map/ppermute | solution.py:339
  47.2 0.7 copy-start.10
  47.2 0.7 copy-start.11
  53.7 0.7 copy-start.3
  53.7 0.8 copy-start.4
  53.7 0.8 copy-start.5
  62.6 27.8 %collective-permute-start.11 = (bf16[8,128,128]{2,1,0:T(8,128)(2,1)}, bf16[8,128,128]{2,1,0:T(8,128)(2,1)S(1)}, u32[]{:S(2)}, u32[]{:S(2)}) collective-permute-start(bf16[8,128,128]{2,1,0:T(8,128)(2,1)} %get-tuple-element.35), channel_id=1, source_target_pairs={{0,8},{8,0},{16,24},{24,16},{1,9},{9,1},{17,25},{25,17},{2,10},{10... | collective-permute-start | bytes 786440 | tf_op jit(solution)/shard_map/ppermute | solution.py:339
  65.5 30.4 %collective-permute-start.12 = (bf16[8,128,128]{2,1,0:T(8,128)(2,1)}, bf16[8,128,128]{2,1,0:T(8,128)(2,1)S(1)}, u32[]{:S(2)}, u32[]{:S(2)}) collective-permute-start(bf16[8,128,128]{2,1,0:T(8,128)(2,1)} %get-tuple-element.36), channel_id=1, source_target_pairs={{0,16},{8,24},{16,0},{24,8},{1,17},{9,25},{17,1},{25,9},{2,18},{10... | collective-permute-start | bytes 786440 | tf_op jit(solution)/shard_map/ppermute | solution.py:339
  67.5 28.4 %collective-permute-start.13 = (bf16[8,128,128]{2,1,0:T(8,128)(2,1)}, bf16[8,128,128]{2,1,0:T(8,128)(2,1)S(1)}, u32[]{:S(2)}, u32[]{:S(2)}) collective-permute-start(bf16[8,128,128]{2,1,0:T(8,128)(2,1)} %get-tuple-element.37), channel_id=1, source_target_pairs={{0,24},{8,16},{16,8},{24,0},{1,25},{9,17},{17,9},{25,1},{2,26},{10... | collective-permute-start | bytes 786440 | tf_op jit(solution)/shard_map/ppermute | solution.py:339
  68.9 1.4 %collective-permute-start.6 = (f32[8,128]{1,0:T(8,128)}, f32[8,128]{1,0:T(8,128)S(1)}, u32[]{:S(2)}, u32[]{:S(2)}) collective-permute-start(f32[8,128]{1,0:T(8,128)} %get-tuple-element.33), channel_id=1, source_target_pairs={{0,1},{1,0},{2,3},{3,2},{4,5},{5,4},{6,7},{7,6},{8,9},{9,8},{10,11... | collective-permute-start | bytes 12296 | tf_op jit(solution)/shard_map/ppermute | solution.py:346
  71.0 3.6 %collective-permute-start.7 = (f32[8,128]{1,0:T(8,128)S(1)}, f32[8,128]{1,0:T(8,128)S(1)}, u32[]{:S(2)}, u32[]{:S(2)}) collective-permute-start(f32[8,128]{1,0:T(8,128)S(1)} %add.15), channel_id=1, source_target_pairs={{0,2},{1,3},{2,0},{3,1},{4,6},{5,7},{6,4},{7,5},{8,10},{9,11},{10,... | collective-permute-start | bytes 12296 | tf_op jit(solution)/shard_map/ppermute | solution.py:346
  74.6 3.6 %collective-permute-start.8 = (f32[8,128]{1,0:T(8,128)S(1)}, f32[8,128]{1,0:T(8,128)S(1)}, u32[]{:S(2)}, u32[]{:S(2)}) collective-permute-start(f32[8,128]{1,0:T(8,128)S(1)} %add.16), channel_id=1, source_target_pairs={{0,4},{1,5},{2,6},{3,7},{4,0},{5,1},{6,2},{7,3},{8,12},{9,13},{10,... | collective-permute-start | bytes 12296 | tf_op jit(solution)/shard_map/ppermute | solution.py:346
  78.2 3.6 %collective-permute-start.9 = (f32[8,128]{1,0:T(8,128)S(1)}, f32[8,128]{1,0:T(8,128)S(1)}, u32[]{:S(2)}, u32[]{:S(2)}) collective-permute-start(f32[8,128]{1,0:T(8,128)S(1)} %add.17), channel_id=1, source_target_pairs={{0,8},{8,0},{16,24},{24,16},{1,9},{9,1},{17,25},{25,17},{2,10},{10... | collective-permute-start | bytes 12296 | tf_op jit(solution)/shard_map/ppermute | solution.py:346
  81.9 8.4 %collective-permute-start.10 = (f32[8,128]{1,0:T(8,128)S(1)}, f32[8,128]{1,0:T(8,128)S(1)}, u32[]{:S(2)}, u32[]{:S(2)}) collective-permute-start(f32[8,128]{1,0:T(8,128)S(1)} %add.18), channel_id=1, source_target_pairs={{0,16},{8,24},{16,0},{24,8},{1,17},{9,25},{17,1},{25,9},{2,18},{10... | collective-permute-start | bytes 12296 | tf_op jit(solution)/shard_map/ppermute | solution.py:346
  85.8 12.9 %collective-permute-start.14 = (bf16[8,80,128]{2,1,0:T(8,128)(2,1)}, bf16[8,80,128]{2,1,0:T(8,128)(2,1)S(1)}, u32[]{:S(2)}, u32[]{:S(2)}) collective-permute-start(bf16[8,80,128]{2,1,0:T(8,128)(2,1)} %get-tuple-element.39), channel_id=1, source_target_pairs={{0,8},{8,0},{16,24},{24,16},{1,9},{9,1},{17,25},{25,17},{2,10},{10... | collective-permute-start | bytes 491528 | tf_op jit(solution)/shard_map/ppermute | solution.py:339
  90.2 12.9 %collective-permute-start.15 = (bf16[8,80,128]{2,1,0:T(8,128)(2,1)}, bf16[8,80,128]{2,1,0:T(8,128)(2,1)S(1)}, u32[]{:S(2)}, u32[]{:S(2)}) collective-permute-start(bf16[8,80,128]{2,1,0:T(8,128)(2,1)} %get-tuple-element.40), channel_id=1, source_target_pairs={{0,16},{8,24},{16,0},{24,8},{1,17},{9,25},{17,1},{25,9},{2,18},{10... | collective-permute-start | bytes 491528 | tf_op jit(solution)/shard_map/ppermute | solution.py:339
  90.4 5.5 %copy-start = (bf16[8,128,128]{2,1,0:T(8,128)(2,1)}, bf16[8,128,128]{2,1,0:T(8,128)(2,1)S(1)}, u32[]{:S(2)}) copy-start(bf16[8,128,128]{2,1,0:T(8,128)(2,1)S(1)} %collective-permute-done.11.refs_1_.refs_2_) | copy-start | bytes 786436
  90.4 12.7 %collective-permute-start.16 = (bf16[8,80,128]{2,1,0:T(8,128)(2,1)}, bf16[8,80,128]{2,1,0:T(8,128)(2,1)S(1)}, u32[]{:S(2)}, u32[]{:S(2)}) collective-permute-start(bf16[8,80,128]{2,1,0:T(8,128)(2,1)} %get-tuple-element.41), channel_id=1, source_target_pairs={{0,24},{8,16},{16,8},{24,0},{1,25},{9,17},{17,9},{25,1},{2,26},{10... | collective-permute-start | bytes 491528 | tf_op jit(solution)/shard_map/ppermute | solution.py:339
  95.9 0.7 copy-start.1
  95.9 0.8 copy-start.2
  98.7 4.5 %copy-start.6 = (bf16[8,80,128]{2,1,0:T(8,128)(2,1)}, bf16[8,80,128]{2,1,0:T(8,128)(2,1)S(1)}, u32[]{:S(2)}) copy-start(bf16[8,80,128]{2,1,0:T(8,128)(2,1)S(1)} %collective-permute-done.14.refs_2_) | copy-start | bytes 491524
  103.1 0.7 copy-start.7
  103.1 0.7 copy-start.8
